TPU v7x, 32 devices: a whole 2x2x4 slice. The times are simulated.
32 devices in a mesh: row: 8 (over z, y), col: 4 (over x, core).
Axes of the slice: x: 2, y: 2, z: 4, core: 2. Of those that a mesh axis runs over, the one named last changes fastest.
Arguments:
- embeddings: float32 [32768, 2048], P('row', 'col'), may hold values from -2.5 to 2.5
- selected: int32 [512], replicated, may hold values from 0 to 32767, as said below
Outputs:
- sample_share: float32 [32768], P(('row', 'col'))
- log_gain: float32 [32768], P(('row', 'col'))
- logdet_mean: float32 [], replicated
Inputs may be any that keep to these rules, and one draw needn't show every extreme that they name: `selected`: 512 distinct item indices.
All inputs are finite; a program needn't handle non-finite values.
Results may differ from a plain program's by a relative error of at most 0.0003.
Values sent between devices are 32-bit elements; how exact they have to be, the bound alone decides.
No kernel may reach another device: no remote copies, remote signals or barrier semaphores. Data moves between devices by JAX's collectives and lax.ppermute only.
A program may use at most 64 MiB of HBM per device.

v0:
```python
import jax
import jax.numpy as jnp
from jax import lax
from jax.sharding import PartitionSpec as P

K = 512


def local(embeddings, selected):
    rows_here = embeddings.shape[0]
    my_index = lax.axis_index("row")
    first_row = my_index * rows_here
    offsets = selected - first_row
    inside = (offsets >= 0) & (offsets < rows_here)
    picked = jnp.take(embeddings, jnp.clip(offsets, 0, rows_here - 1), axis=0)
    picked = jnp.where(inside[:, None], picked, jnp.zeros_like(picked))
    chosen = lax.psum(picked, "row")
    partial_value = jnp.dot(chosen, chosen.T, precision=lax.Precision.HIGHEST)
    kernel = lax.psum(partial_value, "col")
    kernel = kernel + jnp.eye(K, dtype=jnp.float32)
    factor = jnp.linalg.cholesky(kernel)
    logdet_mean = 2.0 * jnp.sum(jnp.log(jnp.diagonal(factor))) / K
    whitened = jax.scipy.linalg.solve_triangular(factor, chosen, lower=True)
    whitened_full = lax.all_gather(whitened, "col", axis=1, tiled=True)
    regrouped = lax.all_to_all(embeddings, "col", split_axis=0, concat_axis=1, tiled=True)
    coordinates = jnp.dot(regrouped, whitened_full.T, precision=lax.Precision.HIGHEST)
    gain = jnp.sum(regrouped * regrouped, axis=1) + 1.0 - jnp.sum(coordinates * coordinates, axis=1)
    item_count = rows_here * lax.axis_size("row")
    grand_total = lax.psum(jnp.sum(gain), ("row", "col"))
    sample_share = gain * (item_count / grand_total)
    return (sample_share, jnp.log(gain), logdet_mean)


def solution(mesh):
    return jax.shard_map(
        local,
        mesh=mesh,
        in_specs=(P("row", "col"), P()),
        out_specs=(P(("row", "col")), P(("row", "col")), P()),
        check_vma=False,
    )
```

profile of v0, /device:TPU:0, one launch (start us, length us, event | category | flops | bytes accessed | tf_op | source)
XLA Modules:
  0.0 403.7 jit_solution(5842791233570516075)
XLA Ops:
  7.2 0.7 compare_and_fusion
  7.9 5.4 %gather_fusion = f32[512,512]{1,0:T(8,128)S(1)} fusion(f32[4096,512]{1,0:T(8,128)} %param.2, s32[1024]{0:T(1024)S(1)} %pad_clamp_fusion), kind=kCustom, calls=%fused_computation | custom fusion | bytes 2099200 | tf_op jit(solution)/shard_map/jit(_take)/gather | solution.py:15
  13.3 1.2 select_select_fusion.1
  14.6 81.2 %all-reduce.4.cloned.1.call-done = f32[512,512]{1,0:T(8,128)} async-done(((f32[512,512]{1,0:T(8,128)}), f32[512,512]{1,0:T(8,128)}) %all-reduce.4.cloned.1.call-update) | async-done | bytes 1048592 | tf_op jit(solution)/shard_map/psum | solution.py:17
  95.8 4.6 %fusion.34 = f32[512,512]{0,1:T(8,128)} fusion(f32[512,512]{1,0:T(8,128)} %all-reduce.4.cloned.1.call-done), kind=kOutput, calls=%fused_computation.85 | convolution fusion | flops 1610612736 | bytes 2097152 | tf_op jit(solution)/shard_map/dot_general | solution.py:18
  100.4 5.7 %all-to-all-start = ((f32[4,1024,512]{2,1,0:T(8,128)}), f32[4,1024,512]{2,1,0:T(8,128)}, u32[]{:S(2)}, u32[]{:S(2)}) async-start(f32[4,1024,512]{2,1,0:T(8,128)} %bitcast.58), calls=%async_computation | async-start | bytes 16777216 | tf_op jit(solution)/shard_map/all_to_all | solution.py:25
  106.1 0.6 all-gather.2.cloned.1.call-start
  106.7 44.8 %all-reduce.6.cloned.1.call-done = f32[512,512]{0,1:T(8,128)} async-done(((f32[512,512]{0,1:T(8,128)}), f32[512,512]{0,1:T(8,128)}) %all-reduce.6.cloned.1.call-update) | async-done | bytes 1048592 | tf_op jit(solution)/shard_map/psum | solution.py:19
  151.5 1.3 convert_add_fusion
  153.1 1.4 fusion
  154.6 1.0 copy-done.1
  155.6 11.7 %cholesky.102 = f32[128,128]{1,0:T(8,128)S(1)} custom-call(f32[128,128]{1,0:T(8,128)S(1)} %cholesky.260), custom_call_target="Cholesky" | custom-call | tf_op jit(solution)/shard_map/jit(cholesky)/cholesky | solution.py:21
  167.3 9.8 %custom-call.31 = f32[1,128,128]{1,2,0:T(8,128)S(1)} custom-call(f32[1,128,128]{2,1,0:T(8,128)S(1)} %get-tuple-element.34), custom_call_target="InvertDiagBlocksLowerTriangular" | custom-call | tf_op jit(solution)/shard_map/jit(cholesky)/cholesky | solution.py:21
  177.3 1.2 constant_dynamic-update-slice_fusion.3
  178.5 1.3 convolution_subtract_fusion.3
  179.8 11.7 %cholesky.213 = f32[128,128]{1,0:T(8,128)S(1)} custom-call(f32[128,128]{1,0:T(8,128)S(1)} %cholesky.264), custom_call_target="Cholesky" | custom-call | tf_op jit(solution)/shard_map/jit(cholesky)/cholesky | solution.py:21
  191.6 10.0 %custom-call.32 = f32[1,128,128]{1,2,0:T(8,128)S(1)} custom-call(f32[1,128,128]{2,1,0:T(8,128)S(1)} %get-tuple-element.31), custom_call_target="InvertDiagBlocksLowerTriangular" | custom-call | tf_op jit(solution)/shard_map/jit(cholesky)/cholesky | solution.py:21
  201.8 1.3 convolution_subtract_fusion.4
  203.1 11.7 %cholesky.234 = f32[128,128]{1,0:T(8,128)S(1)} custom-call(f32[128,128]{1,0:T(8,128)S(1)} %cholesky.269), custom_call_target="Cholesky" | custom-call | tf_op jit(solution)/shard_map/jit(cholesky)/cholesky | solution.py:21
  214.8 0.7 compare_reduce_fusion.1
  215.5 9.8 %custom-call.33 = f32[1,128,128]{1,2,0:T(8,128)S(1)} custom-call(f32[1,128,128]{2,1,0:T(8,128)S(1)} %get-tuple-element.28), custom_call_target="InvertDiagBlocksLowerTriangular" | custom-call | tf_op jit(solution)/shard_map/jit(cholesky)/cholesky | solution.py:21
  225.6 1.2 convolution_subtract_fusion.5
  226.8 11.7 %cholesky.251 = f32[128,128]{1,0:T(8,128)S(1)} custom-call(f32[128,128]{1,0:T(8,128)S(1)} %convolution_subtract_fusion.5), custom_call_target="Cholesky" | custom-call | tf_op jit(solution)/shard_map/jit(cholesky)/cholesky | solution.py:21
  238.5 0.7 compare_reduce_fusion
  239.2 0.8 compare_reduce_fusion.2
  242.7 1.2 fusion.1
  243.9 11.6 %while.1 = (s32[]{:T(128)}, f32[512,512]{1,0:T(8,128)}, s32[4,2]{0,1:T(2,128)S(1)}, f32[4,128,128]{2,1,0:T(8,128)S(1)}, s32[]{:T(128)}) while((s32[]{:T(128)}, f32[512,512]{1,0:T(8,128)}, s32[4,2]{0,1:T(2,128)S(1)}, f32[4,128,128]{2,1,0:T(8,128)S(1)}, s32[]{:T(128)}) %tuple.35), condition=%wide.while_cond, body=%wide.while_body.sunk | while | flops 2 | bytes 131189 | solution.py:23
  244.5 2.3 bitcast_dynamic-update-slice_fusion.2
  246.9 0.5 fusion.45
  247.4 2.3 bitcast_dynamic-update-slice_fusion.2
  249.8 0.5 fusion.45
  250.3 2.3 bitcast_dynamic-update-slice_fusion.2
  252.7 0.5 fusion.45
  253.2 2.2 bitcast_dynamic-update-slice_fusion.2
  255.5 39.3 %custom-call.34 = f32[4,128,128]{1,2,0:T(8,128)S(1)} custom-call(f32[4,128,128]{2,1,0:T(8,128)S(1)} %get-tuple-element.10), custom_call_target="InvertDiagBlocksLowerTriangular" | custom-call | tf_op jit(solution)/shard_map/jit(_solve_triangular)/triangular_solve | solution.py:23
  295.2 1.2 convolution_subtract_fusion.1
  296.9 1.3 convolution_subtract_fusion
  298.7 1.6 convolution_subtract_fusion.2
  300.6 1.0 pad_maximum_fusion
  301.7 4.5 %gather_fusion.1 = f32[512]{0:T(512)S(1)} fusion(f32[512,512]{1,0:T(8,128)S(1)} %get-tuple-element.20, s32[512]{0:T(512)S(1)} %bitcast.57), kind=kCustom, calls=%fused_computation.1 | custom fusion | bytes 8192 | tf_op jit(solution)/shard_map/jit(diagonal)/cond/branch_0_fun/gather | solution.py:22
  306.3 0.6 log_reduce_fusion
  306.9 9.3 %copy.11 = f32[1024,4,512]{0,2,1:T(8,128)} copy(f32[1024,4,512]{2,0,1:T(8,128)} %bitcast.1) | data formatting | bytes 16777216 | tf_op jit(solution)/shard_map/all_to_all | solution.py:25
  316.1 4.0 multiply_reduce_fusion
  320.1 16.2 %all-gather.2.cloned.1.call-done = f32[512,2048]{1,0:T(8,128)} async-done(((f32[512,512]{1,0:T(8,128)}), f32[512,2048]{1,0:T(8,128)}) %all-gather.2.cloned.1.call-update) | async-done | bytes 4194320 | tf_op jit(solution)/shard_map/all_gather | solution.py:24
  336.3 17.4 %multiply_reduce_fusion.1 = f32[1024]{0:T(1024)S(1)} fusion(f32[512,2048]{1,0:T(8,128)} %all-gather.2.cloned.1.call-done, f32[1024,2048]{0,1:T(8,128)} %bitcast.59), kind=kOutput, calls=%fused_computation.5 | convolution fusion | flops 12885949440 | bytes 12587008 | tf_op jit(solution)/shard_map/dot_general | solution.py:26
  353.7 0.6 fusion.32
  355.0 39.5 %psum.23 = f32[]{:T(128)} all-reduce(f32[]{:T(128)} %fusion.32), channel_id=1, replica_groups=mesh['row'=8,'col'=4] {'row','col'}, use_global_device_ids=true, to_apply=%region_13.14 | all-reduce | flops 1 | bytes 8 | tf_op jit(solution)/shard_map/psum | solution.py:29
  395.2 0.6 fusion.31
  (34 shorter events, 3.7 us)
Async XLA Ops:
  7.2 88.6 %all-reduce.4.cloned.1.call-start = ((), (), s32[]{:S(2)}) async-start(), calls=%async_computation.1 | async-start | bytes 2097152 | tf_op jit(solution)/shard_map/psum | solution.py:17
  14.6 136.9 %all-reduce.6.cloned.1.call-start = ((), (), s32[]{:S(2)}) async-start(), calls=%async_computation.2 | async-start | bytes 2097152 | tf_op jit(solution)/shard_map/psum | solution.py:19
  100.4 206.5 %all-to-all-start = ((f32[4,1024,512]{2,1,0:T(8,128)}), f32[4,1024,512]{2,1,0:T(8,128)}, u32[]{:S(2)}, u32[]{:S(2)}) async-start(f32[4,1024,512]{2,1,0:T(8,128)} %bitcast.58), calls=%async_computation | async-start | bytes 16777216 | tf_op jit(solution)/shard_map/all_to_all | solution.py:25
  106.1 188.8 %copy-start = (f32[512,512]{1,0:T(8,128)S(1)}, f32[512,512]{1,0:T(8,128)}, u32[]{:S(2)}) copy-start(f32[512,512]{1,0:T(8,128)} %all-reduce.4.cloned.1.call-done) | copy-start | bytes 3145732
  106.1 230.3 %all-gather.2.cloned.1.call-start = ((), (), s32[]{:S(2)}) async-start(), calls=%async_computation.3 | async-start | bytes 5242880 | tf_op jit(solution)/shard_map/all_gather | solution.py:24
  154.6 1.0 copy-start.1
Sparse Core Ops, SparseCore 0:
  14.7 81.0 all-reduce.3
  100.5 50.9 all-reduce.5
  301.8 34.4 all-gather.1
where the time goes:
time: 408 us; the launch traced here: 404 us
  waiting for transfers between devices  142 us (35%)
  other arithmetic  131 us (32%)
  blocking collectives  39.5 us (10%)
  matrix products  33.2 us (8%)
  local copies, waits for them, and re-layouts  32.1 us (8%)
  between operations  19.4 us (5%)
  starting transfers between devices  6.31 us (2%)
    psum x1, waiting for transfers between devices, local(): chosen = lax.psum(picked, 'row')  81.2 us
    another operation x14, other arithmetic, local(): factor = jnp.linalg.cholesky(kernel)  78.8 us
    psum x1, waiting for transfers between devices, local(): kernel = lax.psum(partial_value, 'col')  44.8 us
    another operation x4, other arithmetic, local(): whitened = jax.scipy.linalg.solve_triangular(factor, chosen, lower=True)  41.6 us
    psum x1, blocking collectives, local(): grand_total = lax.psum(jnp.sum(gain), ('row', 'col'))  39.5 us
    dot_general x1, matrix products, local(): jnp.dot(regrouped, whitened_full.T, precision=lax.Precision.HIGHEST)  17.4 us
    all_gather x1, waiting for transfers between devices, local(): whitened_full = lax.all_gather(whitened, 'col', axis=1, tiled=True)  16.2 us
    another operation x12, local copies, waits for them, and re-layouts  11.5 us
  transfers between devices with their start and end apart: 4, of which 3 were waited for; matrix products, arithmetic and copies ran while one was open for 41% of the time, Pallas kernels for 0%

commit v1 on v0

v1 whole, which is shorter than its diff:
```python
import functools
import math
import jax
import jax.numpy as jnp
from jax import lax
from jax.experimental import pallas as pl
from jax.experimental.pallas import tpu as pltpu
from jax.sharding import PartitionSpec as P

BLOCK = 128
HI = lax.Precision.HIGHEST
GROUP = 32
NEAR = 4


def eliminate(group, first, top, aug):
    tiles = group // 8
    row = lax.broadcasted_iota(jnp.int32, (8, BLOCK), 0)
    full = (8, BLOCK)
    p = [top[8 * t:8 * t + 8] for t in range(tiles)]
    q = [aug[8 * t:8 * t + 8] for t in range(tiles)]
    b = [[jnp.broadcast_to(p[t][:, first + k:first + k + 1], full) for t in range(tiles)] for k in range(group)]
    pivots = [jnp.ones(full, jnp.float32) for _ in range(tiles)]
    for j in range(group):
        tj, sj = divmod(j, 8)
        take = lambda v: jnp.broadcast_to(v[sj:sj + 1, :], full)
        pivot = take(b[j][tj])
        pivots[tj] = jnp.where(row == sj, pivot, pivots[tj])
        if j == group - 1:
            break
        inverse = 1.0 / pivot
        scale = {}
        for t in range(tj, tiles):
            m = b[j][t] * inverse
            scale[t] = jnp.where(row > sj, m, 0.0) if t == tj else m
        ts = [t for t in range(tj, tiles) if not (t == tj and sj == 7)]
        for k in range(j + 1, group):
            r = take(b[k][tj])
            for t in ts:
                b[k][t] = b[k][t] - scale[t] * r
        rp, rq = take(p[tj]), take(q[tj])
        for t in ts:
            p[t] = p[t] - scale[t] * rp
            q[t] = q[t] - scale[t] * rq
    for t in range(tiles):
        s = lax.rsqrt(pivots[t])
        p[t] = p[t] * s
        q[t] = q[t] * s
    logs = sum(jnp.log(v) for v in pivots)
    return jnp.concatenate(p, 0), jnp.concatenate(q, 0), logs


def dot(a, b, contract):
    return lax.dot_general(a, b, ((contract[:1], contract[1:]), ((), ())), precision=HI,
                           preferred_element_type=jnp.float32)


def invert(n, w_ref, d_ref, log_ref):
    r = lax.broadcasted_iota(jnp.int32, (BLOCK, BLOCK), 0)
    c = lax.broadcasted_iota(jnp.int32, (BLOCK, BLOCK), 1)
    eye = (r == c).astype(jnp.float32)
    log_ref[...] = jnp.zeros_like(log_ref)

    def step(k, carry):
        rows = pl.ds(pl.multiple_of(k * BLOCK, BLOCK), BLOCK)
        d_ref[:, :BLOCK] = w_ref[rows, rows]
        d_ref[:, BLOCK:] = eye
        logs = jnp.zeros((8, BLOCK), jnp.float32)
        for lo in range(0, BLOCK, GROUP):
            hi = lo + GROUP
            p, q, part = eliminate(GROUP, lo, d_ref[lo:hi, :BLOCK], d_ref[lo:hi, BLOCK:])
            logs = logs + part
            d_ref[lo:hi, BLOCK:] = q
            if hi < BLOCK:
                change = dot(p, jnp.concatenate([p, q], 1), (0, 0))
                d_ref[hi:, :] = d_ref[hi:, :] - change[hi:]
        log_ref[...] += logs
        window = pl.ds(pl.multiple_of((k + 1) * BLOCK, BLOCK), n)
        x = dot(d_ref[:, BLOCK:], w_ref[rows, window], (1, 0))
        w_ref[rows, window] = x

        def below(i, carry):
            to = pl.ds(pl.multiple_of(i * BLOCK, BLOCK), BLOCK)
            w_ref[to, window] -= dot(w_ref[rows, to], x, (0, 0))
            return carry

        return lax.fori_loop(k + 1, n // BLOCK, below, carry)

    lax.fori_loop(0, n // BLOCK, step, 0)


def identity(n):
    r = lax.broadcasted_iota(jnp.int32, (n, n), 0)
    c = lax.broadcasted_iota(jnp.int32, (n, n), 1)
    return (r == c).astype(jnp.float32)


def pairs(blocks):
    every = [(i, j) for i in range(blocks) for j in range(i, blocks)]
    return every[:len(every) // 2], every[len(every) // 2:]


def split(v, parts=2):
    out = []
    for _ in range(parts):
        out.append(v.astype(jnp.bfloat16))
        v = v - out[-1].astype(jnp.float32)
    return out


def product(a, b, contract):
    n = len(a)
    mul = lambda u, v: lax.dot_general(u, v, ((contract[:1], contract[1:]), ((), ())), preferred_element_type=jnp.float32)
    terms = [mul(a[i], b[k - i]) for k in reversed(range(n)) for i in range(k + 1)]
    return sum(terms[1:], terms[0])


def gram_kernel(core_ref, near_ref, rest_ref, near_other_ref, rest_other_ref, out_ref, *a_refs):
    near, width = near_ref.shape
    for rows, own, other in ((slice(0, near), near_ref, near_other_ref), (slice(near, None), rest_ref, rest_other_ref)):
        for a, u, v in zip(a_refs, split(own[...], 3), split(other[...], 3)):
            a[rows, :width], a[rows, width:] = u, v
    for t, (one, two) in enumerate(zip(*pairs(a_refs[0].shape[0] // BLOCK))):
        i, j = (pl.ds(pl.multiple_of(jnp.where(core_ref[0] == 0, u, v) * BLOCK, BLOCK), BLOCK) for u, v in zip(one, two))
        out_ref[t * BLOCK:(t + 1) * BLOCK, :] = product([a[i, :] for a in a_refs], [a[j, :] for a in a_refs], (1, 1))


def factor_kernel(core_ref, mine_ref, got_ref, inv_ref, log_ref, w_ref, d_ref):
    n = inv_ref.shape[0]
    w_ref[:, n:] = identity(n)
    w_ref[:, :n] = w_ref[:, n:]
    mine = core_ref[0]

    def place(which, ref):
        for t, (i, j) in enumerate(pairs(n // BLOCK)[which]):
            at = slice(i * BLOCK, (i + 1) * BLOCK), slice(j * BLOCK, (j + 1) * BLOCK)
            w_ref[at] = w_ref[at] + ref[t * BLOCK:(t + 1) * BLOCK, :]

    for which in range(2):
        pl.when(mine == which)(functools.partial(place, which, mine_ref))
        pl.when(mine != which)(functools.partial(place, which, got_ref))
    invert(n, w_ref, d_ref, log_ref)
    inv_ref[...] = w_ref[:, n:]


def score_kernel(at_ref, own_ref, other_ref, *refs):
    out_ref, pieces = refs[-1], refs[:-1]
    tile = jnp.concatenate([own_ref[...], other_ref[...]], 1)
    parts = split(tile)
    lo = 0
    for own, other in zip(pieces[::2], pieces[1::2]):
        n = own.shape[0]
        piece = jnp.concatenate([own[...], other[...]], 1)
        if n % BLOCK:
            piece = jnp.concatenate([piece, jnp.zeros((-n % BLOCK, piece.shape[1]), jnp.float32)], 0)
        out_ref[lo:lo + n, :] = jnp.transpose(product(parts, split(piece), (1, 1)))[:n]
        lo += n
    if lo < out_ref.shape[0]:
        squares = jnp.sum(tile * tile, 1, keepdims=True)
        out_ref[lo:, :] = jnp.transpose(jnp.broadcast_to(squares, (squares.shape[0], BLOCK)))[:out_ref.shape[0] - lo]


def score(which, block, embeddings, other_embeddings, norms, *pieces):
    tile = min(512, block)
    steps = block // tile
    items = sum(p.shape[0] for p in pieces[::2]) + (8 if norms else 0)
    width = embeddings.shape[1]
    candidates = pl.BlockSpec((tile, width), lambda i, at: (at[0] * steps + i, 0))
    return pl.pallas_call(
        score_kernel,
        out_shape=f32(items, block),
        grid_spec=pltpu.PrefetchScalarGridSpec(
            num_scalar_prefetch=1,
            grid=(steps,),
            in_specs=[candidates] * 2 + [pl.BlockSpec(p.shape, lambda i, at: (0, 0)) for p in pieces],
            out_specs=pl.BlockSpec((items, tile), lambda i, at: (0, i)),
        ),
        cost_estimate=pl.CostEstimate(flops=4 * items * block * width, bytes_accessed=8 * block * width, transcendentals=0),
    )(which.astype(jnp.int32)[None], embeddings, other_embeddings, *pieces)


def gain_kernel(inv_ref, log_ref, home_ref, near_ref, rest_ref, gain_ref, log_gain_ref, total_ref, *s_refs):
    n, near = inv_ref.shape[0], near_ref.shape[0] - 8
    for rows, got in ((slice(0, near), near_ref), (slice(near, n), rest_ref)):
        for s, v in zip(s_refs, split(home_ref[rows, :] + got[:rows.stop - rows.start, :])):
            s[rows, :] = v
    gain = home_ref[n:n + 1, :] + near_ref[near:near + 1, :] + 1.0
    for lo in range(0, n, BLOCK):
        hi = lo + BLOCK
        along = product(split(inv_ref[lo:hi, :hi]), [s[:hi, :] for s in s_refs], (1, 0))
        gain = gain - jnp.sum(along * along, 0, keepdims=True)
    gain_ref[...] = gain
    log_gain_ref[...] = jnp.log(gain)
    lane = lax.broadcasted_iota(jnp.int32, total_ref.shape, 1)
    logdet = jnp.sum(log_ref[...], 0, keepdims=True)[:, :1] / n
    total_ref[...] = jnp.where(lane == 0, jnp.sum(gain, 1, keepdims=True), logdet)


def share_kernel(count, sums_ref, gain_ref, out_ref, logdet_ref):
    total = jnp.sum(sums_ref[...], 0, keepdims=True)
    out_ref[...] = gain_ref[...] * (count / total[:, :1])
    logdet_ref[...] = sums_ref[:1, 1:2]


def pick_kernel(sel_ref, base_ref, table_ref, out_ref, at_ref, sem):
    slots, rows = out_ref.shape[0], table_ref.shape[0]
    base = base_ref[0]
    step = 16

    def scan(i, count):
        offsets = [sel_ref[i * step + j] - base for j in range(step)]
        inside = [((o >= 0) & (o < rows)).astype(jnp.int32) for o in offsets]
        for o, yes in zip(offsets, inside):
            at_ref[count] = o
            count = count + yes
        return count

    count = lax.fori_loop(0, sel_ref.shape[0] // step, scan, 0)

    def fill(k, carry):
        at_ref[k] = 0
        return carry

    lax.fori_loop(jnp.minimum(count, slots), slots, fill, 0)

    def start(i, carry):
        at = [at_ref[i * 8 + j] for j in range(8)]
        for j in range(8):
            pltpu.make_async_copy(table_ref.at[pl.ds(at[j], 1)], out_ref.at[pl.ds(i * 8 + j, 1)], sem).start()
        return carry

    lax.fori_loop(0, slots // 8, start, 0)
    pltpu.make_async_copy(out_ref, out_ref, sem).wait()


def join_kernel(first, even_ref, source_ref, slow_ref, *refs):
    blocks, out_ref, all_ref = refs[:-2], refs[-2], refs[-1]
    size, n = blocks[0].shape[0], out_ref.shape[0]

    @pl.when(even_ref[0] == 1)
    def _():
        for d, block in enumerate(blocks):
            all_ref[d * size:(d + 1) * size, :] = block[...]

        def copy(i, carry):
            at = [source_ref[i * 8 + j] for j in range(8)]
            out_ref[pl.ds(pl.multiple_of(i * 8, 8), 8), :] = jnp.concatenate([all_ref[pl.ds(a, 1), :] for a in at], 0)
            return carry

        lax.fori_loop(0, n // 8, copy, 0)

    @pl.when(even_ref[0] == 0)
    def _():
        pltpu.sync_copy(slow_ref.at[first:first + n], out_ref)


SMEM, VMEM, ANY = (pl.BlockSpec(memory_space=s) for s in (pltpu.SMEM, pltpu.VMEM, pl.ANY))


def f32(*shape):
    return jax.ShapeDtypeStruct(shape, jnp.float32)


def call(kernel, outs, specs, scratch, flops, *args):
    return pl.pallas_call(
        kernel,
        out_shape=outs,
        in_specs=specs,
        out_specs=(VMEM,) * len(outs) if isinstance(outs, tuple) else VMEM,
        scratch_shapes=scratch,
        cost_estimate=pl.CostEstimate(flops=flops, bytes_accessed=10 ** 6, transcendentals=0),
    )(*args)


def partner(size, distance):
    return [(i, i ^ distance) for i in range(size)]


def tie(value, *after):
    return lax.optimization_barrier((value,) + after)[0]


def any_split(embeddings, offsets):
    n = lax.axis_size("row")
    inside = (offsets >= 0) & (offsets < embeddings.shape[0])
    rows = jnp.take(embeddings, jnp.clip(offsets, 0, embeddings.shape[0] - 1), axis=0)
    rows = jnp.where(inside[:, None], rows, 0.0).reshape(n, -1, embeddings.shape[1])
    share = jnp.sum(lax.all_to_all(rows, "row", 0, 0), 0)
    out = lax.all_to_all(jnp.broadcast_to(share[None], (n,) + share.shape), "row", 0, 0)
    return out.reshape(-1, embeddings.shape[1])


def steps(embeddings, selected):
    rows_here, width = embeddings.shape
    picks = selected.shape[0]
    row_size, col_size = lax.axis_size("row"), lax.axis_size("col")
    row, col = lax.axis_index("row"), lax.axis_index("col")
    core, half = col % 2, col // 2
    block = rows_here // col_size
    to_core = lambda v: lax.ppermute(v, "col", partner(col_size, 1))
    to_chip = lambda v: lax.ppermute(v, "col", partner(col_size, 2))
    to_row = lambda v, s: lax.ppermute(v, "row", partner(row_size, s))
    which_core = core.astype(jnp.int32)[None]

    spread = lambda share: 4.25 * math.sqrt(picks * share * (1 - share))
    slots = min(picks, math.ceil((picks / row_size + spread(1 / row_size)) / 8) * 8)
    near_rows = max(8, int((picks * NEAR / row_size - spread(NEAR / row_size)) / 8) * 8)
    rest_rows = picks - near_rows

    other_embeddings = to_core(embeddings)

    rows = pl.pallas_call(
        pick_kernel,
        out_shape=f32(slots, width),
        in_specs=[SMEM, SMEM, ANY],
        out_specs=VMEM,
        scratch_shapes=[pltpu.SMEM((picks + 8,), jnp.int32), pltpu.SemaphoreType.DMA],
    )(selected, (row * rows_here)[None], embeddings)
    far = [to_row(rows, s) for s in range(NEAR, row_size, NEAR)]
    around = [rows] + [to_row(rows, s) for s in range(1, NEAR)]
    all_far = jnp.concatenate(far, 0)
    beyond = [all_far] + [to_row(all_far, s) for s in range(1, NEAR)]
    beyond = [v[m * slots:(m + 1) * slots] for m in range(len(far)) for v in beyond]

    picked = tie(selected, rows)
    shard = picked // rows_here
    number = jnp.arange(picks)
    before = number[None, :] < number[:, None]
    count = lambda mask: jnp.sum(mask, 1, dtype=jnp.int32)
    rank = count((shard[:, None] == shard[None, :]) & before)
    mine = shard // NEAR == row // NEAR
    place = count(mine[None, :] & (shard[None, :] < shard[:, None])) + rank
    is_near = mine & (place < near_rows)
    place = jnp.where(is_near, place, near_rows + count(before & ~is_near[None, :]))
    found = (shard ^ row) * slots + rank
    source = jnp.sum(jnp.where(place[None, :] == number[:, None], found[None, :], 0), 1)
    source = jnp.clip(source, 0, row_size * slots - 1)
    shards = jnp.arange(row_size)
    counts = count(shard[None, :] == shards[:, None])
    groups = count(shard[None, :] // NEAR == shards[:, None] // NEAR)
    even = jnp.all((counts <= slots) & (groups >= near_rows))
    slow = lax.cond(even, lambda v: jnp.zeros((picks, width), jnp.float32),
                    lambda v: any_split(embeddings, v - row * rows_here), picked)
    even = even.astype(jnp.int32)[None]

    def join(first, n, blocks):
        return call(functools.partial(join_kernel, first), f32(n, width), [SMEM, SMEM, ANY] + [VMEM] * len(blocks),
                    [pltpu.VMEM((len(blocks) * slots, width), jnp.float32)], 10 ** 8,
                    even, source[first:first + n], slow, *blocks)

    away, home = 2 * (1 - half) + core, 2 * half + core
    near = join(0, near_rows, around)
    near_other = to_core(near)
    score_near = score(away, block, embeddings, other_embeddings, True, near, near_other)
    got_near = to_chip(score_near)

    rest = join(near_rows, rest_rows, [tie(v, score_near) for v in around] + beyond)
    rest_other = to_core(rest)
    half_pairs = len(pairs(picks // BLOCK)[0]) * BLOCK
    gram = call(gram_kernel, f32(half_pairs, BLOCK), [SMEM] + [VMEM] * 4, [pltpu.VMEM((picks, 2 * width), jnp.bfloat16)] * 3,
                4 * 10 ** 8, which_core, near, rest, near_other, rest_other)
    gram_got = to_chip(gram)
    rest_t, rest_other_t, _ = lax.optimization_barrier((rest, rest_other, gram))
    score_rest = score(away, block, embeddings, other_embeddings, False, rest_t, rest_other_t)
    got_rest = to_chip(score_rest)
    near_t, near_other_t, _ = lax.optimization_barrier((near, near_other, score_rest))
    score_home = score(home, block, embeddings, other_embeddings, True, near_t, near_other_t, rest_t, rest_other_t)

    gram = tie(gram + gram_got, score_home)
    inverse, logs = call(factor_kernel, (f32(picks, picks), f32(8, BLOCK)), [SMEM] + [VMEM] * 2,
                         [pltpu.VMEM((picks, 2 * picks), jnp.float32), pltpu.VMEM((BLOCK, 2 * BLOCK), jnp.float32)],
                         4 * 10 ** 9, which_core, gram, to_core(gram))

    devices = row_size * col_size
    gain, log_gain, total = call(gain_kernel, (f32(1, block), f32(1, block), f32(devices, BLOCK)), [VMEM] * 5,
                                 [pltpu.VMEM((picks, block), jnp.bfloat16)] * 2, 10 ** 8,
                                 inverse, logs, score_home, got_near, got_rest)
    totals = lax.all_to_all(total.reshape(devices, 1, BLOCK), ("row", "col"), 0, 0).reshape(devices, BLOCK)
    share, logdet = call(functools.partial(share_kernel, rows_here * row_size), (f32(1, block), f32(1, 1)), [VMEM] * 2, [],
                         10 ** 7, totals, gain)
    return (share.reshape(block), log_gain.reshape(block), logdet.reshape(()))


def solution(mesh):
    return jax.shard_map(
        steps,
        mesh=mesh,
        in_specs=(P("row", "col"), P()),
        out_specs=(P(("row", "col")), P(("row", "col")), P()),
        check_vma=False,
    )
```

time: 408 us -> 152 us (0.37)
  other arithmetic: 131 us -> 1.64 us
  waiting for transfers between devices: 142 us -> 48.2 us
  Pallas kernels: 0 us -> 66.2 us
  matrix products: 33.2 us -> 0 us
  blocking collectives: 39.5 us -> 12.6 us
  local copies, waits for them, and re-layouts: 32.1 us -> 7.02 us
  between operations: 19.4 us -> 1.4 us
  starting transfers between devices: 6.31 us -> 14.5 us
    psum x2 -> x0, waiting for transfers between devices: 126 us -> none  [the longest x1 81.2 us: local(): chosen = lax.psum(picked, 'row')]
    another operation x18 -> x0, other arithmetic: 120 us -> none  [the longest x14 78.8 us: local(): factor = jnp.linalg.cholesky(kernel)]
    pallas_call x0 -> x10, Pallas kernels: none -> 66.2 us  [the longest x6 40.3 us: call(): pl.pallas_call(kernel, out_shape=outs, in_specs=specs, out_specs=(VMEM,)...]
    ppermute x0 -> x14, waiting for transfers between devices: none -> 48.2 us  [the longest x3 26 us: steps(): to_chip = lambda v: lax.ppermute(v, 'col', partner(col_size, 2))]
    psum x1 -> x0, blocking collectives: 39.5 us -> none  [local(): grand_total = lax.psum(jnp.sum(gain), ('row', 'col'))]
    dot_general x2 -> x0, matrix products: 21.9 us -> none  [the longest x1 17.4 us: local(): jnp.dot(regrouped, whitened_full.T, precision=lax.Precision.HIGHEST)]
    all_gather x1 -> x0, waiting for transfers between devices: 16.2 us -> none  [local(): whitened_full = lax.all_gather(whitened, 'col', axis=1, tiled=True)]
    ppermute x0 -> x14, starting transfers between devices: none -> 14.5 us  [the longest x7 10.4 us: steps(): to_row = lambda v, s: lax.ppermute(v, 'row', partner(row_size, s))]
  transfers between devices with their start and end apart: 4 -> 14, of which waited for: 3 -> 8; matrix products, arithmetic and copies ran while one was open for 41% -> 2% of each run, Pallas kernels for 0% -> 30%
where the time goes in v1:
time: 152 us
  Pallas kernels  66.2 us (44%)
  waiting for transfers between devices  48.2 us (32%)
  starting transfers between devices  14.5 us (10%)
  blocking collectives  12.6 us (8%)
  local copies, waits for them, and re-layouts  7.02 us (5%)
  other arithmetic  1.64 us (1%)
    pallas_call x6, Pallas kernels, call(): pl.pallas_call(kernel, out_shape=outs, in_specs=specs, out_specs=(VMEM,)...  40.3 us
    ppermute x3, waiting for transfers between devices, steps(): to_chip = lambda v: lax.ppermute(v, 'col', partner(col_size, 2))  26 us
    pallas_call x3, Pallas kernels, score(): pl.pallas_call(score_kernel, out_shape=f32(items, block), grid_spec=pltpu...  20.1 us
    ppermute x7, waiting for transfers between devices, steps(): to_row = lambda v, s: lax.ppermute(v, 'row', partner(row_size, s))  18.3 us
    all_to_all x1, blocking collectives, steps(): lax.all_to_all(total.reshape(devices, 1, BLOCK), ('row', 'col'), 0, 0)  12.6 us
    ppermute x7, starting transfers between devices, steps(): to_row = lambda v, s: lax.ppermute(v, 'row', partner(row_size, s))  10.4 us
    pallas_call x1, Pallas kernels, steps(): pl.pallas_call(pick_kernel, out_shape=f32(slots, width), in_specs=[SMEM,...  5.8 us
    unnamed x32, local copies, waits for them, and re-layouts  5.69 us
  transfers between devices with their start and end apart: 14, of which 8 were waited for; matrix products, arithmetic and copies ran while one was open for 2% of the time, Pallas kernels for 30%

profile of v1, /device:TPU:0, one launch (start us, length us, event | category | flops | bytes accessed | tf_op | source)
XLA Modules:
  0.0 151.7 jit_solution(4666824080514381469)
XLA Ops:
  0.6 0.6 collective-permute-start.3
  1.2 5.8 %shard_map.49.refs_0_ = f32[96,512]{1,0:T(8,128)} custom-call(s32[512]{0:T(512)} %sel_ref.1, s32[1]{0:T(128)} %bitcast.3.base_ref, f32[4096,512]{1,0:T(8,128)} %own_ref.5), custom_call_target="tpu_custom_call" | custom-call | tf_op jit(solution)/shard_map/pallas_call | solution.py:312
  7.0 3.6 %collective-permute-start.2 = (f32[96,512]{1,0:T(8,128)}, f32[96,512]{1,0:T(8,128)S(1)}, u32[]{:S(2)}, u32[]{:S(2)}) collective-permute-start(f32[96,512]{1,0:T(8,128)} %shard_map.49.refs_0_), channel_id=1, source_target_pairs={{0,12},{4,8},{8,4},{12,0},{16,28},{20,24},{24,20},{28,16},{1,13},{... | collective-permute-start | bytes 589832 | tf_op jit(solution)/shard_map/ppermute | solution.py:302
  10.6 0.6 collective-permute-start.1
  11.2 0.1 collective-permute-start
  11.3 0.2 convert_reduce_fusion.3
  11.5 0.6 and_reduce_fusion
  12.8 0.4 convert_reduce_fusion.2
  13.2 0.2 convert_reduce_fusion
  13.4 0.2 select_reduce_fusion
  13.6 0.6 slice.6.source_ref
  14.1 0.1 conditional.1
  14.1 0.1 broadcast.98
  14.3 2.4 %collective-permute-done.2.refs_3_ = f32[96,512]{1,0:T(8,128)S(1)} collective-permute-done((f32[96,512]{1,0:T(8,128)}, f32[96,512]{1,0:T(8,128)S(1)}, u32[]{:S(2)}, u32[]{:S(2)}) %collective-permute-start.2) | collective-permute-done | bytes 196640 | tf_op jit(solution)/shard_map/ppermute | solution.py:302
  16.6 4.3 %collective-permute-done.1.refs_2_ = f32[96,512]{1,0:T(8,128)S(1)} collective-permute-done((f32[96,512]{1,0:T(8,128)}, f32[96,512]{1,0:T(8,128)S(1)}, u32[]{:S(2)}, u32[]{:S(2)}) %collective-permute-start.1) | collective-permute-done | bytes 196640 | tf_op jit(solution)/shard_map/ppermute | solution.py:302
  20.9 0.7 copy-done.7
  21.6 0.1 copy-done.8
  21.7 2.6 %shard_map.50.refs_0_.near_ref = f32[200,512]{1,0:T(8,128)} custom-call(s32[1]{0:T(128)} %bitcast.4.even_ref, s32[200]{0:T(256)} %slice.6.source_ref, f32[512,512]{1,0:T(8,128)S(1)} %get-tuple-element.63.slow_ref, f32[96,512]{1,0:T(8,128)} %shard_map.49.refs_0_, f32[96,512]{1,0:T(8,128)} %copy-done.8, f32[96,512]{1,0:T(8,128)} %copy-done.7, f32[96,512]{1,0:T(8,128)} %copy-done.6), custom_call_target="tpu_custom_call" | custom-call | flops 100000000 | bytes 1000000 | tf_op jit(solution)/shard_map/pallas_call | solution.py:265
  24.3 2.6 %collective-permute-start.5 = (f32[96,512]{1,0:T(8,128)S(1)}, f32[96,512]{1,0:T(8,128)S(1)}, u32[]{:S(2)}, u32[]{:S(2)}) collective-permute-start(f32[96,512]{1,0:T(8,128)S(1)} %copy-done.2), channel_id=1, source_target_pairs={{0,16},{4,20},{8,24},{12,28},{16,0},{20,4},{24,8},{28,12},{1,17},{... | collective-permute-start | bytes 589832 | tf_op jit(solution)/shard_map/ppermute | solution.py:302
  26.9 9.8 %collective-permute-done.5.refs_4_ = f32[96,512]{1,0:T(8,128)S(1)} collective-permute-done((f32[96,512]{1,0:T(8,128)S(1)}, f32[96,512]{1,0:T(8,128)S(1)}, u32[]{:S(2)}, u32[]{:S(2)}) %collective-permute-start.5) | collective-permute-done | bytes 196640 | tf_op jit(solution)/shard_map/ppermute | solution.py:302
  36.7 1.2 collective-permute-start.8
  37.9 1.6 %collective-permute-start.7 = (f32[96,512]{1,0:T(8,128)S(1)}, f32[96,512]{1,0:T(8,128)S(1)}, u32[]{:S(2)}, u32[]{:S(2)}) collective-permute-start(f32[96,512]{1,0:T(8,128)S(1)} %collective-permute-done.5.refs_4_), channel_id=1, source_target_pairs={{0,8},{4,12},{8,0},{12,4},{16,24},{20,28},{24,16},{28,20},{1,9},{5... | collective-permute-start | bytes 589832 | tf_op jit(solution)/shard_map/ppermute | solution.py:302
  39.5 0.7 collective-permute-start.6
  40.2 0.6 slice.7.source_ref
  40.8 0.8 copy-done.1
  41.6 4.7 %shard_map.51 = f32[208,1024]{1,0:T(8,128)} custom-call(s32[1]{0:T(128)} %bitcast.5.at_ref, f32[4096,512]{1,0:T(8,128)} %own_ref.5, f32[4096,512]{1,0:T(8,128)} %collective-permute-done.3.other_ref, f32[200,512]{1,0:T(8,128)} %shard_map.50.refs_0_.near_ref, f32[200,512]{1,0:T(8,128)} %copy-done.1), custom_call_target="tpu_custom_call" | custom-call | flops 436207616 | bytes 4194304 | tf_op jit(solution)/shard_map/pallas_call | solution.py:169
  46.4 1.8 %collective-permute-done.7.refs_6_ = f32[96,512]{1,0:T(8,128)S(1)} collective-permute-done((f32[96,512]{1,0:T(8,128)S(1)}, f32[96,512]{1,0:T(8,128)S(1)}, u32[]{:S(2)}, u32[]{:S(2)}) %collective-permute-start.7) | collective-permute-done | bytes 196640 | tf_op jit(solution)/shard_map/ppermute | solution.py:302
  48.1 0.1 collective-permute-done.6.refs_5_
  48.2 0.6 copy-done.12
  48.8 0.7 copy-done.13
  49.5 3.3 %shard_map.52.rest_ref.refs_0_.refs_2_ = f32[312,512]{1,0:T(8,128)} custom-call(s32[1]{0:T(128)} %bitcast.4.even_ref, s32[312]{0:T(512)} %slice.7.source_ref, f32[512,512]{1,0:T(8,128)S(1)} %get-tuple-element.63.slow_ref, f32[96,512]{1,0:T(8,128)} %shard_map.49.refs_0_, f32[96,512]{1,0:T(8,128)} %copy-done.8, f32[96,512]{1,0:T(8,128)} %copy-done.7, ...), custom_call_target="tpu_custom_call" | custom-call | flops 100000000 | bytes 1000000 | tf_op jit(solution)/shard_map/pallas_call | solution.py:265
  52.8 2.3 %collective-permute-done.9.rest_other_ref.refs_1_.refs_3_ = f32[312,512]{1,0:T(8,128)S(1)} collective-permute-done((f32[312,512]{1,0:T(8,128)}, f32[312,512]{1,0:T(8,128)S(1)}, u32[]{:S(2)}, u32[]{:S(2)}) %collective-permute-start.9) | collective-permute-done | bytes 639008 | tf_op jit(solution)/shard_map/ppermute | solution.py:300
  55.1 0.8 copy-done
  55.9 4.9 %shard_map.53 = f32[640,128]{1,0:T(8,128)} custom-call(s32[1]{0:T(128)} %bitcast.2.core_ref, f32[200,512]{1,0:T(8,128)} %shard_map.50.refs_0_.near_ref, f32[312,512]{1,0:T(8,128)} %shard_map.52.rest_ref.refs_0_.refs_2_, f32[200,512]{1,0:T(8,128)} %copy-done.1, f32[312,512]{1,0:T(8,128)} %copy-done), custom_call_target="tpu_custom_call" | custom-call | flops 400000000 | bytes 1000000 | tf_op jit(solution)/shard_map/pallas_call | solution.py:265
  60.8 6.7 %shard_map.54 = f32[312,1024]{1,0:T(8,128)} custom-call(s32[1]{0:T(128)} %bitcast.5.at_ref, f32[4096,512]{1,0:T(8,128)} %own_ref.5, f32[4096,512]{1,0:T(8,128)} %collective-permute-done.3.other_ref, f32[312,512]{1,0:T(8,128)} %shard_map.52.rest_ref.refs_0_.refs_2_, f32[312,512]{1,0:T(8,128)} %copy-done), custom_call_target="tpu_custom_call" | custom-call | flops 654311424 | bytes 4194304 | tf_op jit(solution)/shard_map/pallas_call | solution.py:169
  67.5 1.5 collective-permute-start.13
  69.0 0.5 collective-permute-start.10
  69.5 1.5 collective-permute-start.12
  71.0 8.7 %shard_map.55.home_ref = f32[520,1024]{1,0:T(8,128)} custom-call(s32[1]{0:T(128)} %bitcast.6.at_ref, f32[4096,512]{1,0:T(8,128)} %own_ref.5, f32[4096,512]{1,0:T(8,128)} %collective-permute-done.3.other_ref, f32[200,512]{1,0:T(8,128)} %shard_map.50.refs_0_.near_ref, f32[200,512]{1,0:T(8,128)} %copy-done.1, f32[312,512]{1,0:T(8,128)} %shard_map.52.rest_ref.refs_0_.refs_2_, ...), custom_call_target="tpu_custom_call" | custom-call | flops 1090519040 | bytes 4194304 | tf_op jit(solution)/shard_map/pallas_call | solution.py:169
  79.7 26.0 %collective-permute-done.10 = f32[640,128]{1,0:T(8,128)S(1)} collective-permute-done((f32[640,128]{1,0:T(8,128)S(1)}, f32[640,128]{1,0:T(8,128)S(1)}, u32[]{:S(2)}, u32[]{:S(2)}) %collective-permute-start.10) | collective-permute-done | bytes 327712 | tf_op jit(solution)/shard_map/ppermute | solution.py:301
  105.8 1.6 %collective-permute-done.11.got_ref = f32[640,128]{1,0:T(8,128)S(1)} collective-permute-done((f32[640,128]{1,0:T(8,128)S(1)}, f32[640,128]{1,0:T(8,128)S(1)}, u32[]{:S(2)}, u32[]{:S(2)}) %collective-permute-start.11) | collective-permute-done | bytes 327712 | tf_op jit(solution)/shard_map/ppermute | solution.py:300
  107.4 0.7 copy-done.15
  108.1 23.5 %shard_map.56 = (f32[512,512]{1,0:T(8,128)}, f32[8,128]{1,0:T(8,128)}) custom-call(s32[1]{0:T(128)} %bitcast.2.core_ref, f32[640,128]{1,0:T(8,128)} %copy-done.9, f32[640,128]{1,0:T(8,128)} %copy-done.15), custom_call_target="tpu_custom_call" | custom-call | flops 4000000000 | bytes 1000000 | tf_op jit(solution)/shard_map/pallas_call | solution.py:265
  131.7 0.9 copy-done.5
  132.5 0.4 copy-done.4
  133.0 4.7 %shard_map.57 = (f32[1,1024]{1,0:T(1,128)}, f32[1,1024]{1,0:T(1,128)}, f32[32,128]{1,0:T(8,128)}) custom-call(f32[512,512]{1,0:T(8,128)} %get-tuple-element.42.inv_ref, f32[8,128]{1,0:T(8,128)} %get-tuple-element.43.log_ref, f32[520,1024]{1,0:T(8,128)} %shard_map.55.home_ref, f32[208,1024]{1,0:T(8,128)} %copy-done.5, f32[312,1024]{1,0:T(8,128)} %copy-done.4), custom_call_target="tpu_custom_call" | custom-call | flops 100000000 | bytes 1000000 | tf_op jit(solution)/shard_map/pallas_call | solution.py:265
  137.6 12.6 %all_to_all.15 = f32[32,1,128]{2,1,0:T(1,128)} all-to-all(f32[32,1,128]{2,1,0:T(1,128)} %bitcast.16), channel_id=1, replica_groups=mesh['row'=8,'col'=4] {'row','col'}, dimensions={0} | all-to-all | bytes 32768 | tf_op jit(solution)/shard_map/all_to_all | solution.py:378
  150.3 1.4 shard_map.58
  (38 shorter events, 0.2 us)
Async XLA Ops:
  0.6 10.7 %copy-start.14 = (s32[512]{0:T(512)S(1)}, s32[512]{0:T(512)}, u32[]{:S(2)}) copy-start(s32[512]{0:T(512)} %sel_ref.1) | copy-start | bytes 6148
  0.6 40.2 %collective-permute-start.3 = (f32[4096,512]{1,0:T(8,128)}, f32[4096,512]{1,0:T(8,128)}, u32[]{:S(2)}, u32[]{:S(2)}) collective-permute-start(f32[4096,512]{1,0:T(8,128)} %own_ref.5), channel_id=1, source_target_pairs={{0,1},{1,0},{2,3},{3,2},{4,5},{5,4},{6,7},{7,6},{8,9},{9,8},{10,11... | collective-permute-start | bytes 25165832 | tf_op jit(solution)/shard_map/ppermute | solution.py:300
  7.0 9.6 %collective-permute-start.2 = (f32[96,512]{1,0:T(8,128)}, f32[96,512]{1,0:T(8,128)S(1)}, u32[]{:S(2)}, u32[]{:S(2)}) collective-permute-start(f32[96,512]{1,0:T(8,128)} %shard_map.49.refs_0_), channel_id=1, source_target_pairs={{0,12},{4,8},{8,4},{12,0},{16,28},{20,24},{24,20},{28,16},{1,13},{... | collective-permute-start | bytes 589832 | tf_op jit(solution)/shard_map/ppermute | solution.py:302
  10.6 10.3 %collective-permute-start.1 = (f32[96,512]{1,0:T(8,128)}, f32[96,512]{1,0:T(8,128)S(1)}, u32[]{:S(2)}, u32[]{:S(2)}) collective-permute-start(f32[96,512]{1,0:T(8,128)} %shard_map.49.refs_0_), channel_id=1, source_target_pairs={{0,8},{4,12},{8,0},{12,4},{16,24},{20,28},{24,16},{28,20},{1,9},{5... | collective-permute-start | bytes 589832 | tf_op jit(solution)/shard_map/ppermute | solution.py:302
  11.2 9.7 %collective-permute-start = (f32[96,512]{1,0:T(8,128)}, f32[96,512]{1,0:T(8,128)S(1)}, u32[]{:S(2)}, u32[]{:S(2)}) collective-permute-start(f32[96,512]{1,0:T(8,128)} %shard_map.49.refs_0_), channel_id=1, source_target_pairs={{0,4},{4,0},{8,12},{12,8},{16,20},{20,16},{24,28},{28,24},{1,5},{5... | collective-permute-start | bytes 589832 | tf_op jit(solution)/shard_map/ppermute | solution.py:302
  14.1 10.1 %copy-start.2 = (f32[96,512]{1,0:T(8,128)S(1)}, f32[96,512]{1,0:T(8,128)}, u32[]{:S(2)}) copy-start(f32[96,512]{1,0:T(8,128)} %shard_map.49.refs_0_) | copy-start | bytes 589828
  16.6 4.3 %copy-start.6 = (f32[96,512]{1,0:T(8,128)}, f32[96,512]{1,0:T(8,128)S(1)}, u32[]{:S(2)}) copy-start(f32[96,512]{1,0:T(8,128)S(1)} %collective-permute-done.2.refs_3_) | copy-start | bytes 589828
  20.9 0.7 copy-start.7
  20.9 0.7 copy-start.8
  24.3 16.6 %collective-permute-start.4 = (f32[200,512]{1,0:T(8,128)}, f32[200,512]{1,0:T(8,128)S(1)}, u32[]{:S(2)}, u32[]{:S(2)}) collective-permute-start(f32[200,512]{1,0:T(8,128)} %shard_map.50.refs_0_.near_ref), channel_id=1, source_target_pairs={{0,1},{1,0},{2,3},{3,2},{4,5},{5,4},{6,7},{7,6},{8,9},{9,8},{10,11... | collective-permute-start | bytes 1228808 | tf_op jit(solution)/shard_map/ppermute | solution.py:300
  24.3 12.4 %collective-permute-start.5 = (f32[96,512]{1,0:T(8,128)S(1)}, f32[96,512]{1,0:T(8,128)S(1)}, u32[]{:S(2)}, u32[]{:S(2)}) collective-permute-start(f32[96,512]{1,0:T(8,128)S(1)} %copy-done.2), channel_id=1, source_target_pairs={{0,16},{4,20},{8,24},{12,28},{16,0},{20,4},{24,8},{28,12},{1,17},{... | collective-permute-start | bytes 589832 | tf_op jit(solution)/shard_map/ppermute | solution.py:302
  36.7 11.5 %copy-start.10 = (f32[96,512]{1,0:T(8,128)}, f32[96,512]{1,0:T(8,128)S(1)}, u32[]{:S(2)}) copy-start(f32[96,512]{1,0:T(8,128)S(1)} %collective-permute-done.5.refs_4_) | copy-start | bytes 589828
  36.7 9.7 %collective-permute-start.8 = (f32[96,512]{1,0:T(8,128)S(1)}, f32[96,512]{1,0:T(8,128)S(1)}, u32[]{:S(2)}, u32[]{:S(2)}) collective-permute-start(f32[96,512]{1,0:T(8,128)S(1)} %collective-permute-done.5.refs_4_), channel_id=1, source_target_pairs={{0,12},{4,8},{8,4},{12,0},{16,28},{20,24},{24,20},{28,16},{1,13},{... | collective-permute-start | bytes 589832 | tf_op jit(solution)/shard_map/ppermute | solution.py:302
  37.9 10.2 %collective-permute-start.7 = (f32[96,512]{1,0:T(8,128)S(1)}, f32[96,512]{1,0:T(8,128)S(1)}, u32[]{:S(2)}, u32[]{:S(2)}) collective-permute-start(f32[96,512]{1,0:T(8,128)S(1)} %collective-permute-done.5.refs_4_), channel_id=1, source_target_pairs={{0,8},{4,12},{8,0},{12,4},{16,24},{20,28},{24,16},{28,20},{1,9},{5... | collective-permute-start | bytes 589832 | tf_op jit(solution)/shard_map/ppermute | solution.py:302
  39.5 8.7 %collective-permute-start.6 = (f32[96,512]{1,0:T(8,128)S(1)}, f32[96,512]{1,0:T(8,128)S(1)}, u32[]{:S(2)}, u32[]{:S(2)}) collective-permute-start(f32[96,512]{1,0:T(8,128)S(1)} %collective-permute-done.5.refs_4_), channel_id=1, source_target_pairs={{0,4},{4,0},{8,12},{12,8},{16,20},{20,16},{24,28},{28,24},{1,5},{5... | collective-permute-start | bytes 589832 | tf_op jit(solution)/shard_map/ppermute | solution.py:302
  40.8 0.8 copy-start.1
  46.4 1.8 %copy-start.11 = (f32[96,512]{1,0:T(8,128)}, f32[96,512]{1,0:T(8,128)S(1)}, u32[]{:S(2)}) copy-start(f32[96,512]{1,0:T(8,128)S(1)} %collective-permute-done.8.refs_7_) | copy-start | bytes 589828
  48.1 0.7 copy-start.12
  48.8 0.7 copy-start.13
  52.8 2.3 %collective-permute-start.9 = (f32[312,512]{1,0:T(8,128)}, f32[312,512]{1,0:T(8,128)S(1)}, u32[]{:S(2)}, u32[]{:S(2)}) collective-permute-start(f32[312,512]{1,0:T(8,128)} %shard_map.52.rest_ref.refs_0_.refs_2_), channel_id=1, source_target_pairs={{0,1},{1,0},{2,3},{3,2},{4,5},{5,4},{6,7},{7,6},{8,9},{9,8},{10,11... | collective-permute-start | bytes 1916936 | tf_op jit(solution)/shard_map/ppermute | solution.py:300
  55.1 0.8 copy-start
  60.8 8.2 %copy-start.3 = (f32[640,128]{1,0:T(8,128)S(1)}, f32[640,128]{1,0:T(8,128)}, u32[]{:S(2)}) copy-start(f32[640,128]{1,0:T(8,128)} %shard_map.53) | copy-start | bytes 983044
  67.5 64.2 %collective-permute-start.13 = (f32[312,1024]{1,0:T(8,128)}, f32[312,1024]{1,0:T(8,128)S(1)}, u32[]{:S(2)}, u32[]{:S(2)}) collective-permute-start(f32[312,1024]{1,0:T(8,128)} %shard_map.54), channel_id=1, source_target_pairs={{0,2},{1,3},{2,0},{3,1},{4,6},{5,7},{6,4},{7,5},{8,10},{9,11},{10,... | collective-permute-start | bytes 3833864 | tf_op jit(solution)/shard_map/ppermute | solution.py:301
  69.0 36.7 %collective-permute-start.10 = (f32[640,128]{1,0:T(8,128)S(1)}, f32[640,128]{1,0:T(8,128)S(1)}, u32[]{:S(2)}, u32[]{:S(2)}) collective-permute-start(f32[640,128]{1,0:T(8,128)S(1)} %copy-done.3), channel_id=1, source_target_pairs={{0,2},{1,3},{2,0},{3,1},{4,6},{5,7},{6,4},{7,5},{8,10},{9,11},{10,... | collective-permute-start | bytes 983048 | tf_op jit(solution)/shard_map/ppermute | solution.py:301
  69.5 62.1 %collective-permute-start.12 = (f32[208,1024]{1,0:T(8,128)}, f32[208,1024]{1,0:T(8,128)S(1)}, u32[]{:S(2)}, u32[]{:S(2)}) collective-permute-start(f32[208,1024]{1,0:T(8,128)} %shard_map.51), channel_id=1, source_target_pairs={{0,2},{1,3},{2,0},{3,1},{4,6},{5,7},{6,4},{7,5},{8,10},{9,11},{10,... | collective-permute-start | bytes 2555912 | tf_op jit(solution)/shard_map/ppermute | solution.py:301
  105.7 1.7 %copy-start.9 = (f32[640,128]{1,0:T(8,128)}, f32[640,128]{1,0:T(8,128)S(1)}, u32[]{:S(2)}) copy-start(f32[640,128]{1,0:T(8,128)S(1)} %add.45.mine_ref) | copy-start | bytes 983044
  105.7 1.7 %collective-permute-start.11 = (f32[640,128]{1,0:T(8,128)S(1)}, f32[640,128]{1,0:T(8,128)S(1)}, u32[]{:S(2)}, u32[]{:S(2)}) collective-permute-start(f32[640,128]{1,0:T(8,128)S(1)} %add.45.mine_ref), channel_id=1, source_target_pairs={{0,1},{1,0},{2,3},{3,2},{4,5},{5,4},{6,7},{7,6},{8,9},{9,8},{10,11... | collective-permute-start | bytes 983048 | tf_op jit(solution)/shard_map/ppermute | solution.py:300
  107.4 0.7 copy-start.15
  131.6 0.9 copy-start.5
  131.7 1.3 copy-start.4

commit v2 on v1

--- a/solution.py
+++ b/solution.py
@@ -143,48 +143,73 @@
     inv_ref[...] = w_ref[:, n:]
 
 
-def score_kernel(at_ref, own_ref, other_ref, *refs):
-    out_ref, pieces = refs[-1], refs[:-1]
-    tile = jnp.concatenate([own_ref[...], other_ref[...]], 1)
-    parts = split(tile)
-    lo = 0
+def prepare_kernel(at_ref, own_ref, other_ref, high_ref, low_ref, norm_ref, tile_ref, sems):
+    size, width = tile_ref.shape[1], own_ref.shape[1]
+    count = high_ref.shape[0] // size
+
+    def copies(t):
+        rows = pl.ds(pl.multiple_of(at_ref[0] + t * size, size), size)
+        return [pltpu.make_async_copy(ref.at[rows], tile_ref.at[t % 2, :, side * width:(side + 1) * width], sems.at[t % 2, side])
+                for side, ref in enumerate((own_ref, other_ref))]
+
+    def start(t):
+        for copy in copies(t):
+            copy.start()
+
+    start(0)
+    for t in range(count):
+        if t + 1 < count:
+            start(t + 1)
+        for copy in copies(t):
+            copy.wait()
+        tile = tile_ref[t % 2]
+        rows = slice(t * size, (t + 1) * size)
+        high_ref[rows, :], low_ref[rows, :] = split(tile)
+        squares = jnp.sum(tile * tile, 1, keepdims=True)
+        norm_ref[:, rows] = jnp.transpose(jnp.broadcast_to(squares, (size, BLOCK)))[:8]
+
+
+def score_kernel(high_ref, low_ref, *refs):
+    *pieces, out_ref = refs
+    norms = [pieces.pop()] if len(pieces) % 2 else []
+    size = min(512, high_ref.shape[0])
+    selected = []
     for own, other in zip(pieces[::2], pieces[1::2]):
-        n = own.shape[0]
         piece = jnp.concatenate([own[...], other[...]], 1)
-        if n % BLOCK:
-            piece = jnp.concatenate([piece, jnp.zeros((-n % BLOCK, piece.shape[1]), jnp.float32)], 0)
-        out_ref[lo:lo + n, :] = jnp.transpose(product(parts, split(piece), (1, 1)))[:n]
-        lo += n
-    if lo < out_ref.shape[0]:
-        squares = jnp.sum(tile * tile, 1, keepdims=True)
-        out_ref[lo:, :] = jnp.transpose(jnp.broadcast_to(squares, (squares.shape[0], BLOCK)))[:out_ref.shape[0] - lo]
-
-
-def score(which, block, embeddings, other_embeddings, norms, *pieces):
-    tile = min(512, block)
-    steps = block // tile
-    items = sum(p.shape[0] for p in pieces[::2]) + (8 if norms else 0)
-    width = embeddings.shape[1]
-    candidates = pl.BlockSpec((tile, width), lambda i, at: (at[0] * steps + i, 0))
-    return pl.pallas_call(
-        score_kernel,
-        out_shape=f32(items, block),
-        grid_spec=pltpu.PrefetchScalarGridSpec(
-            num_scalar_prefetch=1,
-            grid=(steps,),
-            in_specs=[candidates] * 2 + [pl.BlockSpec(p.shape, lambda i, at: (0, 0)) for p in pieces],
-            out_specs=pl.BlockSpec((items, tile), lambda i, at: (0, i)),
-        ),
-        cost_estimate=pl.CostEstimate(flops=4 * items * block * width, bytes_accessed=8 * block * width, transcendentals=0),
-    )(which.astype(jnp.int32)[None], embeddings, other_embeddings, *pieces)
-
-
-def gain_kernel(inv_ref, log_ref, home_ref, near_ref, rest_ref, gain_ref, log_gain_ref, total_ref, *s_refs):
+        if own.shape[0] % BLOCK:
+            piece = jnp.concatenate([piece, jnp.zeros((-own.shape[0] % BLOCK, piece.shape[1]), jnp.float32)], 0)
+        selected.append((own.shape[0], split(piece)))
+    for t in range(high_ref.shape[0] // size):
+        rows = slice(t * size, (t + 1) * size)
+        parts = [high_ref[rows, :], low_ref[rows, :]]
+        lo = 0
+        for n, piece in selected:
+            out_ref[lo:lo + n, rows] = jnp.transpose(product(parts, piece, (1, 1)))[:n]
+            lo += n
+    for norm in norms:
+        out_ref[lo:, :] = norm[...]
+
+
+def prepare(which, block, embeddings, other_embeddings):
+    tile, width = min(256, block), embeddings.shape[1]
+    part = jax.ShapeDtypeStruct((block, 2 * width), jnp.bfloat16)
+    return call(prepare_kernel, (part, part, f32(8, block)), [SMEM, ANY, ANY],
+                [pltpu.VMEM((2, tile, 2 * width), jnp.float32), pltpu.SemaphoreType.DMA((2, 2))],
+                10 ** 9, (which * block).astype(jnp.int32)[None], embeddings, other_embeddings)
+
+
+def score(prepared, *pieces):
+    block, items = prepared[0].shape[0], sum(p.shape[0] for p in pieces[::2]) + (8 if len(prepared) > 2 else 0)
+    return call(score_kernel, f32(items, block), [VMEM] * (len(pieces) + len(prepared)), [], 10 ** 9,
+                *prepared[:2], *pieces, *prepared[2:])
+
+
+def gain_kernel(inv_ref, log_ref, norm_ref, home_ref, near_ref, rest_ref, gain_ref, log_gain_ref, total_ref, *s_refs):
     n, near = inv_ref.shape[0], near_ref.shape[0] - 8
     for rows, got in ((slice(0, near), near_ref), (slice(near, n), rest_ref)):
         for s, v in zip(s_refs, split(home_ref[rows, :] + got[:rows.stop - rows.start, :])):
             s[rows, :] = v
-    gain = home_ref[n:n + 1, :] + near_ref[near:near + 1, :] + 1.0
+    gain = norm_ref[:1, :] + near_ref[near:near + 1, :] + 1.0
     for lo in range(0, n, BLOCK):
         hi = lo + BLOCK
         along = product(split(inv_ref[lo:hi, :hi]), [s[:hi, :] for s in s_refs], (1, 0))
@@ -243,7 +268,7 @@
             all_ref[d * size:(d + 1) * size, :] = block[...]
 
         def copy(i, carry):
-            at = [source_ref[i * 8 + j] for j in range(8)]
+            at = [source_ref[first + i * 8 + j] for j in range(8)]
             out_ref[pl.ds(pl.multiple_of(i * 8, 8), 8), :] = jnp.concatenate([all_ref[pl.ds(a, 1), :] for a in at], 0)
             return carry
 
@@ -259,6 +284,9 @@
 
 def f32(*shape):
     return jax.ShapeDtypeStruct(shape, jnp.float32)
+
+
+GRANT = pltpu.CompilerParams(vmem_limit_bytes=20 * 2 ** 20)
 
 
 def call(kernel, outs, specs, scratch, flops, *args):
@@ -269,6 +297,7 @@
         out_specs=(VMEM,) * len(outs) if isinstance(outs, tuple) else VMEM,
         scratch_shapes=scratch,
         cost_estimate=pl.CostEstimate(flops=flops, bytes_accessed=10 ** 6, transcendentals=0),
+        compiler_params=GRANT,
     )(*args)
 
 
@@ -315,6 +344,7 @@
         in_specs=[SMEM, SMEM, ANY],
         out_specs=VMEM,
         scratch_shapes=[pltpu.SMEM((picks + 8,), jnp.int32), pltpu.SemaphoreType.DMA],
+        compiler_params=GRANT,
     )(selected, (row * rows_here)[None], embeddings)
     far = [to_row(rows, s) for s in range(NEAR, row_size, NEAR)]
     around = [rows] + [to_row(rows, s) for s in range(1, NEAR)]
@@ -346,12 +376,12 @@
     def join(first, n, blocks):
         return call(functools.partial(join_kernel, first), f32(n, width), [SMEM, SMEM, ANY] + [VMEM] * len(blocks),
                     [pltpu.VMEM((len(blocks) * slots, width), jnp.float32)], 10 ** 8,
-                    even, source[first:first + n], slow, *blocks)
-
-    away, home = 2 * (1 - half) + core, 2 * half + core
+                    even, source, slow, *blocks)
+
+    away = prepare(2 * (1 - half) + core, block, embeddings, other_embeddings)
     near = join(0, near_rows, around)
     near_other = to_core(near)
-    score_near = score(away, block, embeddings, other_embeddings, True, near, near_other)
+    score_near = score(away, near, near_other)
     got_near = to_chip(score_near)
 
     rest = join(near_rows, rest_rows, [tie(v, score_near) for v in around] + beyond)
@@ -361,10 +391,11 @@
                 4 * 10 ** 8, which_core, near, rest, near_other, rest_other)
     gram_got = to_chip(gram)
     rest_t, rest_other_t, _ = lax.optimization_barrier((rest, rest_other, gram))
-    score_rest = score(away, block, embeddings, other_embeddings, False, rest_t, rest_other_t)
+    score_rest = score(away[:2], rest_t, rest_other_t)
     got_rest = to_chip(score_rest)
     near_t, near_other_t, _ = lax.optimization_barrier((near, near_other, score_rest))
-    score_home = score(home, block, embeddings, other_embeddings, True, near_t, near_other_t, rest_t, rest_other_t)
+    home = prepare(2 * half + core, block, tie(embeddings, score_rest), other_embeddings)
+    score_home = score(home[:2], near_t, near_other_t, rest_t, rest_other_t)
 
     gram = tie(gram + gram_got, score_home)
     inverse, logs = call(factor_kernel, (f32(picks, picks), f32(8, BLOCK)), [SMEM] + [VMEM] * 2,
@@ -372,9 +403,9 @@
                          4 * 10 ** 9, which_core, gram, to_core(gram))
 
     devices = row_size * col_size
-    gain, log_gain, total = call(gain_kernel, (f32(1, block), f32(1, block), f32(devices, BLOCK)), [VMEM] * 5,
+    gain, log_gain, total = call(gain_kernel, (f32(1, block), f32(1, block), f32(devices, BLOCK)), [VMEM] * 6,
                                  [pltpu.VMEM((picks, block), jnp.bfloat16)] * 2, 10 ** 8,
-                                 inverse, logs, score_home, got_near, got_rest)
+                                 inverse, logs, home[2], score_home, got_near, got_rest)
     totals = lax.all_to_all(total.reshape(devices, 1, BLOCK), ("row", "col"), 0, 0).reshape(devices, BLOCK)
     share, logdet = call(functools.partial(share_kernel, rows_here * row_size), (f32(1, block), f32(1, 1)), [VMEM] * 2, [],
                          10 ** 7, totals, gain)

time: 152 us -> 140 us (0.921)
  Pallas kernels: 66.2 us -> 54.9 us
  local copies, waits for them, and re-layouts: 7.02 us -> 4.94 us
    pallas_call x3 -> x0, Pallas kernels: 20.1 us -> none  [score(): pl.pallas_call(score_kernel, out_shape=f32(items, block), grid_spec=pltpu...]
    pallas_call x6 -> x11, Pallas kernels: 40.3 us -> 49.6 us  [call(): pl.pallas_call(kernel, out_shape=outs, in_specs=specs, out_specs=(VMEM,)...]
    unnamed x32 -> x18, local copies, waits for them, and re-layouts: 5.69 us -> 4.83 us
  transfers between devices with their start and end apart: 14 -> 14, of which waited for: 8 -> 7; matrix products, arithmetic and copies ran while one was open for 2% -> 2% of each run, Pallas kernels for 30% -> 30%
where the time goes in v2:
time: 140 us; the launch traced here: 139 us
  Pallas kernels  54.9 us (39%)
  waiting for transfers between devices  48.5 us (35%)
  starting transfers between devices  14.8 us (11%)
  blocking collectives  12.2 us (9%)
  local copies, waits for them, and re-layouts  4.94 us (4%)
  other arithmetic  2.62 us (2%)
  between operations  1.48 us (1%)
    pallas_call x11, Pallas kernels, call(): pl.pallas_call(kernel, out_shape=outs, in_specs=specs, out_specs=(VMEM,)...  49.6 us
    ppermute x3, waiting for transfers between devices, steps(): to_chip = lambda v: lax.ppermute(v, 'col', partner(col_size, 2))  26.2 us
    ppermute x7, waiting for transfers between devices, steps(): to_row = lambda v, s: lax.ppermute(v, 'row', partner(row_size, s))  18.6 us
    all_to_all x1, blocking collectives, steps(): lax.all_to_all(total.reshape(devices, 1, BLOCK), ('row', 'col'), 0, 0)  12.2 us
    ppermute x7, starting transfers between devices, steps(): to_row = lambda v, s: lax.ppermute(v, 'row', partner(row_size, s))  10.5 us
    pallas_call x1, Pallas kernels, steps(): pl.pallas_call(pick_kernel, out_shape=f32(slots, width), in_specs=[SMEM,...  5.25 us
    unnamed x18, local copies, waits for them, and re-layouts  4.83 us
    ppermute x4, waiting for transfers between devices, steps(): to_core = lambda v: lax.ppermute(v, 'col', partner(col_size, 1))  3.68 us
  transfers between devices with their start and end apart: 14, of which 7 were waited for; matrix products, arithmetic and copies ran while one was open for 2% of the time, Pallas kernels for 30%

profile of v2, /device:TPU:0, one launch (start us, length us, event | category | flops | bytes accessed | tf_op | source)
XLA Modules:
  0.0 139.4 jit_solution(8881624197310222654)
XLA Ops:
  0.6 0.6 collective-permute-start.3
  1.2 5.2 %shard_map.49.refs_0_ = f32[96,512]{1,0:T(8,128)S(1)} custom-call(s32[512]{0:T(512)} %sel_ref.1, s32[1]{0:T(128)} %bitcast.3.base_ref, f32[4096,512]{1,0:T(8,128)} %own_ref.2), custom_call_target="tpu_custom_call" | custom-call | tf_op jit(solution)/shard_map/pallas_call | solution.py:341
  6.4 3.7 %collective-permute-start.2 = (f32[96,512]{1,0:T(8,128)S(1)}, f32[96,512]{1,0:T(8,128)S(1)}, u32[]{:S(2)}, u32[]{:S(2)}) collective-permute-start(f32[96,512]{1,0:T(8,128)S(1)} %shard_map.49.refs_0_), channel_id=1, source_target_pairs={{0,12},{4,8},{8,4},{12,0},{16,28},{20,24},{24,20},{28,16},{1,13},{... | collective-permute-start | bytes 589832 | tf_op jit(solution)/shard_map/ppermute | solution.py:331
  10.1 0.6 collective-permute-start.1
  10.7 0.1 collective-permute-start
  10.8 0.2 convert_reduce_fusion.3
  11.0 0.6 and_reduce_fusion
  12.2 0.1 conditional.1
  12.3 0.1 broadcast.98
  12.4 0.4 convert_reduce_fusion.2
  12.8 0.2 convert_reduce_fusion
  13.0 0.2 select_reduce_fusion
  13.2 2.7 %collective-permute-done.2.refs_3_ = f32[96,512]{1,0:T(8,128)S(1)} collective-permute-done((f32[96,512]{1,0:T(8,128)S(1)}, f32[96,512]{1,0:T(8,128)S(1)}, u32[]{:S(2)}, u32[]{:S(2)}) %collective-permute-start.2) | collective-permute-done | bytes 196640 | tf_op jit(solution)/shard_map/ppermute | solution.py:331
  15.9 4.3 %collective-permute-done.1.refs_2_ = f32[96,512]{1,0:T(8,128)S(1)} collective-permute-done((f32[96,512]{1,0:T(8,128)S(1)}, f32[96,512]{1,0:T(8,128)S(1)}, u32[]{:S(2)}, u32[]{:S(2)}) %collective-permute-start.1) | collective-permute-done | bytes 196640 | tf_op jit(solution)/shard_map/ppermute | solution.py:331
  20.2 1.2 shard_map.50.refs_0_.near_ref
  21.3 0.1 collective-permute-start.4
  21.4 2.7 %collective-permute-start.5 = (f32[96,512]{1,0:T(8,128)S(1)}, f32[96,512]{1,0:T(8,128)S(1)}, u32[]{:S(2)}, u32[]{:S(2)}) collective-permute-start(f32[96,512]{1,0:T(8,128)S(1)} %shard_map.49.refs_0_), channel_id=1, source_target_pairs={{0,16},{4,20},{8,24},{12,28},{16,0},{20,4},{24,8},{28,12},{1,17},{... | collective-permute-start | bytes 589832 | tf_op jit(solution)/shard_map/ppermute | solution.py:331
  24.1 9.7 %collective-permute-done.5.refs_4_ = f32[96,512]{1,0:T(8,128)S(1)} collective-permute-done((f32[96,512]{1,0:T(8,128)S(1)}, f32[96,512]{1,0:T(8,128)S(1)}, u32[]{:S(2)}, u32[]{:S(2)}) %collective-permute-start.5) | collective-permute-done | bytes 196640 | tf_op jit(solution)/shard_map/ppermute | solution.py:331
  33.8 1.3 collective-permute-start.8
  35.1 1.6 %collective-permute-start.7 = (f32[96,512]{1,0:T(8,128)S(1)}, f32[96,512]{1,0:T(8,128)S(1)}, u32[]{:S(2)}, u32[]{:S(2)}) collective-permute-start(f32[96,512]{1,0:T(8,128)S(1)} %collective-permute-done.5.refs_4_), channel_id=1, source_target_pairs={{0,8},{4,12},{8,0},{12,4},{16,24},{20,28},{24,16},{28,20},{1,9},{5... | collective-permute-start | bytes 589832 | tf_op jit(solution)/shard_map/ppermute | solution.py:331
  36.7 0.6 collective-permute-start.6
  37.3 3.3 %shard_map.51 = (bf16[1024,1024]{1,0:T(8,128)(2,1)S(1)}, bf16[1024,1024]{1,0:T(8,128)(2,1)S(1)}, f32[8,1024]{1,0:T(8,128)S(1)}) custom-call(s32[1]{0:T(128)} %bitcast.5.at_ref, f32[4096,512]{1,0:T(8,128)} %own_ref.2, f32[4096,512]{1,0:T(8,128)} %collective-permute-done.3.other_ref), custom_call_target="tpu_custom_call" | custom-call | flops 1000000000 | bytes 1000000 | tf_op jit(solution)/shard_map/pallas_call | solution.py:293
  40.7 2.0 %shard_map.52 = f32[208,1024]{1,0:T(8,128)S(1)} custom-call(bf16[1024,1024]{1,0:T(8,128)(2,1)S(1)} %get-tuple-element.40.high_ref, bf16[1024,1024]{1,0:T(8,128)(2,1)S(1)} %get-tuple-element.41.low_ref, f32[200,512]{1,0:T(8,128)S(1)} %shard_map.50.refs_0_.near_ref, f32[200,512]{1,0:T(8,128)S(1)} %collective-permute-done.4.refs_1_.near_other_ref, ...), custom_call_target="tpu_custom_call" | custom-call | flops 1000000000 | bytes 1000000 | tf_op jit(solution)/shard_map/pallas_call | solution.py:293
  42.7 0.7 copy-done
  43.4 1.9 %collective-permute-done.7.refs_6_ = f32[96,512]{1,0:T(8,128)S(1)} collective-permute-done((f32[96,512]{1,0:T(8,128)S(1)}, f32[96,512]{1,0:T(8,128)S(1)}, u32[]{:S(2)}, u32[]{:S(2)}) %collective-permute-start.7) | collective-permute-done | bytes 196640 | tf_op jit(solution)/shard_map/ppermute | solution.py:331
  45.3 0.7 copy-done.2
  46.0 0.7 copy-done.4
  46.7 0.9 copy-done.1
  47.6 0.9 copy-done.3
  48.5 0.9 copy-done.5
  49.5 1.7 %shard_map.53.rest_ref.refs_0_.refs_2_ = f32[312,512]{1,0:T(8,128)S(1)} custom-call(s32[1]{0:T(128)} %bitcast.4.even_ref, s32[512]{0:T(512)S(1)} %broadcast_clamp_fusion.source_ref, f32[512,512]{1,0:T(8,128)S(1)} %copy-done.7, f32[96,512]{1,0:T(8,128)S(1)} %shard_map.49.refs_0_, f32[96,512]{1,0:T(8,128)S(1)} %collective-permute-done.refs_1_, ...), custom_call_target="tpu_custom_call" | custom-call | flops 100000000 | bytes 1000000 | tf_op jit(solution)/shard_map/pallas_call | solution.py:293
  51.1 0.1 collective-permute-start.9
  51.2 2.1 %collective-permute-done.9.rest_other_ref.refs_1_.refs_3_ = f32[312,512]{1,0:T(8,128)S(1)} collective-permute-done((f32[312,512]{1,0:T(8,128)S(1)}, f32[312,512]{1,0:T(8,128)S(1)}, u32[]{:S(2)}, u32[]{:S(2)}) %collective-permute-start.9) | collective-permute-done | bytes 639008 | tf_op jit(solution)/shard_map/ppermute | solution.py:329
  53.3 2.6 %shard_map.54 = f32[640,128]{1,0:T(8,128)S(1)} custom-call(s32[1]{0:T(128)} %bitcast.2.core_ref, f32[200,512]{1,0:T(8,128)S(1)} %shard_map.50.refs_0_.near_ref, f32[312,512]{1,0:T(8,128)S(1)} %shard_map.53.rest_ref.refs_0_.refs_2_, f32[200,512]{1,0:T(8,128)S(1)} %collective-permute-done.4.refs_1_.near_other_ref, ...), custom_call_target="tpu_custom_call" | custom-call | flops 400000000 | bytes 1000000 | tf_op jit(solution)/shard_map/pallas_call | solution.py:293
  55.9 4.7 %shard_map.55 = f32[312,1024]{1,0:T(8,128)} custom-call(bf16[1024,1024]{1,0:T(8,128)(2,1)S(1)} %get-tuple-element.40.high_ref, bf16[1024,1024]{1,0:T(8,128)(2,1)S(1)} %get-tuple-element.41.low_ref, f32[312,512]{1,0:T(8,128)S(1)} %shard_map.53.rest_ref.refs_0_.refs_2_, f32[312,512]{1,0:T(8,128)S(1)} %collective-permute-done.9.rest_other_ref.refs_1_.refs_3_), custom_call_target="tpu_custom_call" | custom-call | flops 1000000000 | bytes 1000000 | tf_op jit(solution)/shard_map/pallas_call | solution.py:293
  60.6 1.5 %collective-permute-start.13 = (f32[312,1024]{1,0:T(8,128)}, f32[312,1024]{1,0:T(8,128)}, u32[]{:S(2)}, u32[]{:S(2)}) collective-permute-start(f32[312,1024]{1,0:T(8,128)} %shard_map.55), channel_id=1, source_target_pairs={{0,2},{1,3},{2,0},{3,1},{4,6},{5,7},{6,4},{7,5},{8,10},{9,11},{10,... | collective-permute-start | bytes 3833864 | tf_op jit(solution)/shard_map/ppermute | solution.py:330
  62.1 0.5 collective-permute-start.10
  62.7 1.5 %collective-permute-start.12 = (f32[208,1024]{1,0:T(8,128)S(1)}, f32[208,1024]{1,0:T(8,128)S(1)}, u32[]{:S(2)}, u32[]{:S(2)}) collective-permute-start(f32[208,1024]{1,0:T(8,128)S(1)} %shard_map.52), channel_id=1, source_target_pairs={{0,2},{1,3},{2,0},{3,1},{4,6},{5,7},{6,4},{7,5},{8,10},{9,11},{10,... | collective-permute-start | bytes 2555912 | tf_op jit(solution)/shard_map/ppermute | solution.py:330
  64.2 3.3 %shard_map.56 = (bf16[1024,1024]{1,0:T(8,128)(2,1)S(1)}, bf16[1024,1024]{1,0:T(8,128)(2,1)S(1)}, f32[8,1024]{1,0:T(8,128)S(1)}) custom-call(s32[1]{0:T(128)} %bitcast.6.at_ref, f32[4096,512]{1,0:T(8,128)} %own_ref.2, f32[4096,512]{1,0:T(8,128)} %collective-permute-done.3.other_ref), custom_call_target="tpu_custom_call" | custom-call | flops 1000000000 | bytes 1000000 | tf_op jit(solution)/shard_map/pallas_call | solution.py:293
  67.5 5.2 %shard_map.57.home_ref = f32[512,1024]{1,0:T(8,128)S(1)} custom-call(bf16[1024,1024]{1,0:T(8,128)(2,1)S(1)} %get-tuple-element.50.high_ref, bf16[1024,1024]{1,0:T(8,128)(2,1)S(1)} %get-tuple-element.51.low_ref, f32[200,512]{1,0:T(8,128)S(1)} %shard_map.50.refs_0_.near_ref, f32[200,512]{1,0:T(8,128)S(1)} %collective-permute-done.4.refs_1_.near_other_ref, ...), custom_call_target="tpu_custom_call" | custom-call | flops 1000000000 | bytes 1000000 | tf_op jit(solution)/shard_map/pallas_call | solution.py:293
  72.7 26.2 %collective-permute-done.10 = f32[640,128]{1,0:T(8,128)} collective-permute-done((f32[640,128]{1,0:T(8,128)S(1)}, f32[640,128]{1,0:T(8,128)}, u32[]{:S(2)}, u32[]{:S(2)}) %collective-permute-start.10) | collective-permute-done | bytes 327712 | tf_op jit(solution)/shard_map/ppermute | solution.py:330
  98.9 1.0 add.45.mine_ref
  99.9 0.1 collective-permute-start.11
  100.0 1.6 %collective-permute-done.11.got_ref = f32[640,128]{1,0:T(8,128)S(1)} collective-permute-done((f32[640,128]{1,0:T(8,128)S(1)}, f32[640,128]{1,0:T(8,128)S(1)}, u32[]{:S(2)}, u32[]{:S(2)}) %collective-permute-start.11) | collective-permute-done | bytes 327712 | tf_op jit(solution)/shard_map/ppermute | solution.py:329
  101.6 21.5 %shard_map.58 = (f32[512,512]{1,0:T(8,128)S(1)}, f32[8,128]{1,0:T(8,128)S(1)}) custom-call(s32[1]{0:T(128)} %bitcast.2.core_ref, f32[640,128]{1,0:T(8,128)S(1)} %add.45.mine_ref, f32[640,128]{1,0:T(8,128)S(1)} %collective-permute-done.11.got_ref), custom_call_target="tpu_custom_call" | custom-call | flops 4000000000 | bytes 1000000 | tf_op jit(solution)/shard_map/pallas_call | solution.py:293
  123.2 3.4 %shard_map.59 = (f32[1,1024]{1,0:T(1,128)S(1)}, f32[1,1024]{1,0:T(1,128)}, f32[32,128]{1,0:T(8,128)S(1)}) custom-call(f32[512,512]{1,0:T(8,128)S(1)} %get-tuple-element.55.inv_ref, f32[8,128]{1,0:T(8,128)S(1)} %get-tuple-element.56.log_ref, f32[8,1024]{1,0:T(8,128)S(1)} %get-tuple-element.57.norm_ref, f32[512,1024]{1,0:T(8,128)S(1)} %shard_map.57.home_ref, ...), custom_call_target="tpu_custom_call" | custom-call | flops 100000000 | bytes 1000000 | tf_op jit(solution)/shard_map/pallas_call | solution.py:293
  126.6 12.2 %all_to_all.15 = f32[32,1,128]{2,1,0:T(1,128)S(1)} all-to-all(f32[32,1,128]{2,1,0:T(1,128)S(1)} %bitcast.14), channel_id=1, replica_groups=mesh['row'=8,'col'=4] {'row','col'}, dimensions={0} | all-to-all | bytes 32768 | tf_op jit(solution)/shard_map/all_to_all | solution.py:409
  138.8 0.7 shard_map.60
  (24 shorter events, 0.1 us)
Async XLA Ops:
  0.6 36.7 %collective-permute-start.3 = (f32[4096,512]{1,0:T(8,128)}, f32[4096,512]{1,0:T(8,128)}, u32[]{:S(2)}, u32[]{:S(2)}) collective-permute-start(f32[4096,512]{1,0:T(8,128)} %own_ref.2), channel_id=1, source_target_pairs={{0,1},{1,0},{2,3},{3,2},{4,5},{5,4},{6,7},{7,6},{8,9},{9,8},{10,11... | collective-permute-start | bytes 25165832 | tf_op jit(solution)/shard_map/ppermute | solution.py:329
  1.2 9.6 %copy-start.8 = (s32[512]{0:T(512)S(1)}, s32[512]{0:T(512)}, u32[]{:S(2)}) copy-start(s32[512]{0:T(512)} %sel_ref.1) | copy-start | bytes 6148
  6.4 9.4 %collective-permute-start.2 = (f32[96,512]{1,0:T(8,128)S(1)}, f32[96,512]{1,0:T(8,128)S(1)}, u32[]{:S(2)}, u32[]{:S(2)}) collective-permute-start(f32[96,512]{1,0:T(8,128)S(1)} %shard_map.49.refs_0_), channel_id=1, source_target_pairs={{0,12},{4,8},{8,4},{12,0},{16,28},{20,24},{24,20},{28,16},{1,13},{... | collective-permute-start | bytes 589832 | tf_op jit(solution)/shard_map/ppermute | solution.py:331
  10.1 10.1 %collective-permute-start.1 = (f32[96,512]{1,0:T(8,128)S(1)}, f32[96,512]{1,0:T(8,128)S(1)}, u32[]{:S(2)}, u32[]{:S(2)}) collective-permute-start(f32[96,512]{1,0:T(8,128)S(1)} %shard_map.49.refs_0_), channel_id=1, source_target_pairs={{0,8},{4,12},{8,0},{12,4},{16,24},{20,28},{24,16},{28,20},{1,9},{5... | collective-permute-start | bytes 589832 | tf_op jit(solution)/shard_map/ppermute | solution.py:331
  10.7 9.5 %collective-permute-start = (f32[96,512]{1,0:T(8,128)S(1)}, f32[96,512]{1,0:T(8,128)S(1)}, u32[]{:S(2)}, u32[]{:S(2)}) collective-permute-start(f32[96,512]{1,0:T(8,128)S(1)} %shard_map.49.refs_0_), channel_id=1, source_target_pairs={{0,4},{4,0},{8,12},{12,8},{16,20},{20,16},{24,28},{28,24},{1,5},{5... | collective-permute-start | bytes 589832 | tf_op jit(solution)/shard_map/ppermute | solution.py:331
  12.4 8.9 %copy-start.6 = (f32[512,512]{1,0:T(8,128)}, f32[512,512]{1,0:T(8,128)S(1)}, u32[]{:S(2)}) copy-start(f32[512,512]{1,0:T(8,128)S(1)} %get-tuple-element.77.slow_ref) | copy-start | bytes 3145732
  21.3 19.3 %collective-permute-start.4 = (f32[200,512]{1,0:T(8,128)S(1)}, f32[200,512]{1,0:T(8,128)S(1)}, u32[]{:S(2)}, u32[]{:S(2)}) collective-permute-start(f32[200,512]{1,0:T(8,128)S(1)} %shard_map.50.refs_0_.near_ref), channel_id=1, source_target_pairs={{0,1},{1,0},{2,3},{3,2},{4,5},{5,4},{6,7},{7,6},{8,9},{9,8},{10,11... | collective-permute-start | bytes 1228808 | tf_op jit(solution)/shard_map/ppermute | solution.py:329
  21.4 12.4 %collective-permute-start.5 = (f32[96,512]{1,0:T(8,128)S(1)}, f32[96,512]{1,0:T(8,128)S(1)}, u32[]{:S(2)}, u32[]{:S(2)}) collective-permute-start(f32[96,512]{1,0:T(8,128)S(1)} %shard_map.49.refs_0_), channel_id=1, source_target_pairs={{0,16},{4,20},{8,24},{12,28},{16,0},{20,4},{24,8},{28,12},{1,17},{... | collective-permute-start | bytes 589832 | tf_op jit(solution)/shard_map/ppermute | solution.py:331
  33.8 8.9 %collective-permute-start.8 = (f32[96,512]{1,0:T(8,128)S(1)}, f32[96,512]{1,0:T(8,128)S(1)}, u32[]{:S(2)}, u32[]{:S(2)}) collective-permute-start(f32[96,512]{1,0:T(8,128)S(1)} %collective-permute-done.5.refs_4_), channel_id=1, source_target_pairs={{0,12},{4,8},{8,4},{12,0},{16,28},{20,24},{24,20},{28,16},{1,13},{... | collective-permute-start | bytes 589832 | tf_op jit(solution)/shard_map/ppermute | solution.py:331
  35.1 10.2 %collective-permute-start.7 = (f32[96,512]{1,0:T(8,128)S(1)}, f32[96,512]{1,0:T(8,128)S(1)}, u32[]{:S(2)}, u32[]{:S(2)}) collective-permute-start(f32[96,512]{1,0:T(8,128)S(1)} %collective-permute-done.5.refs_4_), channel_id=1, source_target_pairs={{0,8},{4,12},{8,0},{12,4},{16,24},{20,28},{24,16},{28,20},{1,9},{5... | collective-permute-start | bytes 589832 | tf_op jit(solution)/shard_map/ppermute | solution.py:331
  36.7 9.3 %collective-permute-start.6 = (f32[96,512]{1,0:T(8,128)S(1)}, f32[96,512]{1,0:T(8,128)S(1)}, u32[]{:S(2)}, u32[]{:S(2)}) collective-permute-start(f32[96,512]{1,0:T(8,128)S(1)} %collective-permute-done.5.refs_4_), channel_id=1, source_target_pairs={{0,4},{4,0},{8,12},{12,8},{16,20},{20,16},{24,28},{28,24},{1,5},{5... | collective-permute-start | bytes 589832 | tf_op jit(solution)/shard_map/ppermute | solution.py:331
  40.7 6.0 %copy-start.7 = (f32[512,512]{1,0:T(8,128)S(1)}, f32[512,512]{1,0:T(8,128)}, u32[]{:S(2)}) copy-start(f32[512,512]{1,0:T(8,128)} %copy-done.6) | copy-start | bytes 3145732
  42.7 0.7 copy-start
  45.3 0.7 copy-start.2
  46.0 0.7 copy-start.4
  46.7 0.9 copy-start.1
  47.6 0.9 copy-start.3
  48.5 0.9 copy-start.5
  51.1 2.1 %collective-permute-start.9 = (f32[312,512]{1,0:T(8,128)S(1)}, f32[312,512]{1,0:T(8,128)S(1)}, u32[]{:S(2)}, u32[]{:S(2)}) collective-permute-start(f32[312,512]{1,0:T(8,128)S(1)} %shard_map.53.rest_ref.refs_0_.refs_2_), channel_id=1, source_target_pairs={{0,1},{1,0},{2,3},{3,2},{4,5},{5,4},{6,7},{7,6},{8,9},{9,8},{10,11... | collective-permute-start | bytes 1916936 | tf_op jit(solution)/shard_map/ppermute | solution.py:329
  60.6 62.5 %collective-permute-start.13 = (f32[312,1024]{1,0:T(8,128)}, f32[312,1024]{1,0:T(8,128)}, u32[]{:S(2)}, u32[]{:S(2)}) collective-permute-start(f32[312,1024]{1,0:T(8,128)} %shard_map.55), channel_id=1, source_target_pairs={{0,2},{1,3},{2,0},{3,1},{4,6},{5,7},{6,4},{7,5},{8,10},{9,11},{10,... | collective-permute-start | bytes 3833864 | tf_op jit(solution)/shard_map/ppermute | solution.py:330
  62.1 36.8 %collective-permute-start.10 = (f32[640,128]{1,0:T(8,128)S(1)}, f32[640,128]{1,0:T(8,128)}, u32[]{:S(2)}, u32[]{:S(2)}) collective-permute-start(f32[640,128]{1,0:T(8,128)S(1)} %shard_map.54), channel_id=1, source_target_pairs={{0,2},{1,3},{2,0},{3,1},{4,6},{5,7},{6,4},{7,5},{8,10},{9,11},{10,... | collective-permute-start | bytes 983048 | tf_op jit(solution)/shard_map/ppermute | solution.py:330
  62.7 60.5 %collective-permute-start.12 = (f32[208,1024]{1,0:T(8,128)S(1)}, f32[208,1024]{1,0:T(8,128)S(1)}, u32[]{:S(2)}, u32[]{:S(2)}) collective-permute-start(f32[208,1024]{1,0:T(8,128)S(1)} %shard_map.52), channel_id=1, source_target_pairs={{0,2},{1,3},{2,0},{3,1},{4,6},{5,7},{6,4},{7,5},{8,10},{9,11},{10,... | collective-permute-start | bytes 2555912 | tf_op jit(solution)/shard_map/ppermute | solution.py:330
  99.9 1.7 %collective-permute-start.11 = (f32[640,128]{1,0:T(8,128)S(1)}, f32[640,128]{1,0:T(8,128)S(1)}, u32[]{:S(2)}, u32[]{:S(2)}) collective-permute-start(f32[640,128]{1,0:T(8,128)S(1)} %add.45.mine_ref), channel_id=1, source_target_pairs={{0,1},{1,0},{2,3},{3,2},{4,5},{5,4},{6,7},{7,6},{8,9},{9,8},{10,11... | collective-permute-start | bytes 983048 | tf_op jit(solution)/shard_map/ppermute | solution.py:329
